TPU v7x, 256 devices: a 2x2x32 block of a 4x8x32 slice. The times are simulated.
256 devices in a mesh: grp: 4 (over x, y), tp: 32 (over z), tower: 2 (over core).
Axes of the slice: x: 2, y: 2, z: 32, core: 2. Of those that a mesh axis runs over, the one named last changes fastest.
The devices are a block of a 4x8x32 slice.
Arguments:
- hidden: bfloat16 [2, 4096, 3072], P('tower', ('grp', 'tp')), parts along dimension 1, may hold values from -6 to 6
- modulation: float32 [2, 3, 3072], P('tower'), may hold values from -3 to 7, as said below
- qk_gains: float32 [2, 3, 4096], P('tower', None, 'tp'), may hold values from 0.75 to 13
- counts: int32 [2, 4], P(None, 'grp'), parts along dimension 1, may hold values from 256 to 1024
- offsets: int32 [2, 4], P(None, 'grp'), parts along dimension 1, may hold values from 0 to 8191
- in_weights: bfloat16 [2, 3072, 4, 4096], P('tower', None, None, 'tp'), may hold values from -0.109375 to 0.109375
- out_weights: bfloat16 [2, 2, 4096, 3072], P('tower', None, 'tp'), may hold values from -0.5 to 0.5
Outputs:
- updated: bfloat16 [2, 4096, 3072], P('tower', ('grp', 'tp')), parts along dimension 1
There are 4 independent parts, one for each index of `grp`. A program takes and returns all parts, laid end to end along the dimension named above; an argument that names none is the same for every part. Nothing has to cross between parts.
Inputs may be any that keep to these rules, and one draw needn't show every extreme that they name: `modulation`: rows are shift, scale and gate.
All inputs are finite; a program needn't handle non-finite values.
Results may differ from a plain program's by a relative error of at most 0.025.
The roundings to bfloat16 on the way count: a program that leaves them out, or rounds other values in their place, can miss the bound.
Values may be sent and summed in bfloat16 or wider, within the bound.
A program may use at most 64 MiB of HBM per device.

v0:
```python
import math

import jax
import jax.numpy as jnp
from jax import lax
from jax.sharding import PartitionSpec as P

epsilon = 1e-06
rope_base = 10000.0
masked_score = -1e30


def partner(value, axis, distance):
    mask = 2**distance
    pairs = [(source, source ^ mask) for source in range(lax.axis_size(axis))]
    return lax.ppermute(value, axis, pairs)


def layer_norm(states):
    centre = states - jnp.mean(states, -1, keepdims=True)
    spread = jnp.mean(centre * centre, -1, keepdims=True)
    return centre * lax.rsqrt(spread + epsilon)


def rotate(columns, positions):
    head_width = columns.shape[-1]
    pair_index = jnp.arange(head_width // 2, dtype=jnp.int32)
    frequency = jnp.exp(pair_index.astype(jnp.float32) * (-2.0 * math.log(rope_base) / head_width))
    angles = positions.reshape((positions.shape[0],) + (1,) * (columns.ndim - 1)) * frequency
    cosine = jnp.cos(angles)
    sine_table = jnp.sin(angles)
    even_part = columns[..., 0::2]
    odd_part = columns[..., 1::2]
    turned = jnp.stack(
        [even_part * cosine - odd_part * sine_table, even_part * sine_table + odd_part * cosine], -1
    )
    return turned.reshape(columns.shape)


def finish(projected, head_gains, positions):
    query_like = jnp.stack([projected[:, 0], projected[:, 1], projected[:, 3]], 1)
    squares = jnp.mean(query_like * query_like, -1, keepdims=True)
    query_like = query_like * lax.rsqrt(squares + epsilon) * head_gains[None]
    turned = rotate(query_like, positions)
    return jnp.stack([turned[:, 0], turned[:, 1], projected[:, 2], turned[:, 2]], 1)


def attend(queries, key_rows, value_rows, key_count):
    scores = jnp.einsum("qd,kd->qk", queries, key_rows, preferred_element_type=jnp.float32) * (
        1.0 / math.sqrt(queries.shape[-1])
    )
    usable = jnp.arange(key_rows.shape[0], dtype=jnp.int32) < key_count
    scores = jnp.where(usable[None, :], scores, masked_score)
    row_max = jnp.max(scores, -1, keepdims=True)
    raised = jnp.exp(scores - row_max)
    attention = (raised / jnp.sum(raised, -1, keepdims=True)).astype(jnp.bfloat16)
    return jnp.dot(attention, value_rows, preferred_element_type=jnp.float32).astype(jnp.bfloat16)


def attend_blocks(queries, key_rows, value_rows, key_count):
    row_count = queries.shape[0]
    block_rows = min(512, row_count)
    grouped = queries.reshape(row_count // block_rows, block_rows, queries.shape[-1])
    result = lax.map(
        lambda query_block: attend(query_block, key_rows, value_rows, key_count), grouped
    )
    return result.reshape(row_count, queries.shape[-1])


def local(hidden, modulation, qk_gains, counts, offsets, in_weights, out_weights):
    states = hidden[0].astype(jnp.float32)
    modulate = modulation[0]
    normed = (layer_norm(states) * (1.0 + modulate[1]) + modulate[0]).astype(jnp.bfloat16)
    local_rows = states.shape[0]
    model_width = normed.shape[1]
    all_rows = local_rows * lax.axis_size("tp")
    tower_index = lax.axis_index("tower")
    own_count = lax.dynamic_index_in_dim(counts[:, 0], tower_index, 0, False)
    own_offset = lax.dynamic_index_in_dim(offsets[:, 0], tower_index, 0, False)
    head_width = in_weights.shape[-1]
    flat_weights = in_weights[0].reshape(model_width, 4 * head_width)
    head_gains = qk_gains[0].reshape(3, 1, head_width)
    row_piece = lax.all_gather(normed, "tp", axis=0, tiled=True)
    row_count = row_piece.shape[0]
    projected = jnp.dot(row_piece, flat_weights, preferred_element_type=jnp.float32).reshape(
        row_count, 4, 1, head_width
    )
    positions = (own_offset + jnp.arange(row_count, dtype=jnp.int32)).astype(jnp.float32)
    finished = finish(projected, head_gains, positions)
    projected = (
        finished.astype(jnp.bfloat16)
        .reshape(row_count, 4 * head_width)
        .reshape(all_rows, 4, head_width)
    )
    queries = projected[:, 0]
    key_rows = projected[:, 1]
    value_rows = projected[:, 2]
    cross_queries = projected[:, 3]
    self_out = attend_blocks(queries, key_rows, value_rows, own_count)
    foreign = partner(cross_queries, "tower", 0)
    answered = attend_blocks(foreign, key_rows, value_rows, own_count)
    cross_out = partner(answered, "tower", 0)
    both_out = jnp.concatenate([self_out, cross_out], 1)
    flat_out = out_weights[0].reshape(2 * head_width, model_width)
    branch = lax.psum_scatter(
        jnp.dot(both_out, flat_out, preferred_element_type=jnp.float32).astype(jnp.bfloat16),
        "tp",
        scatter_dimension=0,
        tiled=True,
    ).astype(jnp.float32)
    return (states + modulate[2] * branch).astype(jnp.bfloat16)[None]


def solution(mesh):
    return jax.shard_map(
        local,
        mesh=mesh,
        in_specs=(
            P("tower", ("grp", "tp"), None),
            P("tower", None, None),
            P("tower", None, "tp"),
            P(None, "grp"),
            P(None, "grp"),
            P("tower", None, None, "tp"),
            P("tower", None, "tp", None),
        ),
        out_specs=P("tower", ("grp", "tp"), None),
        check_vma=False,
    )
```

profile of v0, /device:TPU:38, one launch (start us, length us, event | category | flops | bytes accessed | tf_op | source)
XLA Modules:
  0.0 345.4 jit_solution(10798262315295197064)
XLA Ops:
  6.6 0.9 fusion.41
  7.4 1.1 convert_reduce_fusion
  8.5 1.2 fusion.32
  9.7 1.8 fusion.35
  11.6 4.1 %copy.25 = bf16[384,8,4,128]{3,1,2,0:T(8,128)(2,1)} copy(bf16[384,8,4,128]{3,2,1,0:T(4,128)(2,1)} %bitcast.111) | data formatting | bytes 6291456
  15.6 4.8 %copy.11 = bf16[512,3072]{1,0:T(8,128)(2,1)} copy(bf16[512,3072]{0,1:T(8,128)(2,1)} %bitcast.108) | data formatting | bytes 6291456 | tf_op jit(solution)/shard_map/dot_general | solution.py:85
  22.3 1.8 multiply_cosine_fusion
  24.1 142.7 %all-gather.2.cloned.1.call-done = bf16[1024,3072]{1,0:T(8,128)(2,1)} async-done(((bf16[32,3072]{1,0:T(8,128)(2,1)}), bf16[1024,3072]{1,0:T(8,128)(2,1)}) %all-gather.2.cloned.1.call-update) | async-done | bytes 6291472 | tf_op jit(solution)/shard_map/all_gather | solution.py:83
  166.8 6.5 %fusion.22 = f32[1024,4,1,128]{0,3,1,2:T(8,128)S(1)} fusion(bf16[4,128,3072]{2,1,0:T(8,128)(2,1)} %bitcast.112, bf16[1024,3072]{1,0:T(8,128)(2,1)} %all-gather.2.cloned.1.call-done), kind=kOutput, calls=%fused_computation.34 | convolution fusion | flops 3221225472 | bytes 11534336 | tf_op jit(solution)/shard_map/dot_general | solution.py:85
  173.6 1.1 copy-done.2
  174.9 2.2 slice.56
  177.1 2.1 slice.55
  179.2 1.7 subtract_bitcast_fusion
  181.0 0.8 copy.12
  182.6 1.1 fusion.37
  184.2 5.1 %while.21 = (s32[]{:T(128)}, bf16[2,512,128]{2,1,0:T(8,128)(2,1)S(1)}, s32[]{:T(128)}, bf16[2,512,128]{2,1,0:T(8,128)(2,1)S(1)}, bf16[1024,128]{1,0:T(8,128)(2,1)S(1)}, /*index=5*/bf16[1024,128]{1,0:T(8,128)(2,1)S(1)}, s32[]{:T(128)}) while((s32[]{:T(128)}, bf16[2,512,128]{2,1,0:T(8,128)(2,1)S(1)}, s32[]{:T(128)}, ...), condition=%wide.region_10.11_spmd, body=%wide.region_7.10_spmd.sunk | while | flops 274792448 | bytes 7092321 | solution.py:64
  186.1 0.7 fusion.67
  188.6 0.7 fusion.67
  189.3 0.8 collective-permute-start.1
  190.2 5.1 %while.20 = (s32[]{:T(128)}, bf16[2,512,128]{2,1,0:T(8,128)(2,1)S(1)}, s32[]{:T(128)}, bf16[2,512,128]{2,1,0:T(8,128)(2,1)S(1)}, bf16[1024,128]{1,0:T(8,128)(2,1)S(1)}, /*index=5*/bf16[1024,128]{1,0:T(8,128)(2,1)S(1)}, s32[]{:T(128)}) while((s32[]{:T(128)}, bf16[2,512,128]{2,1,0:T(8,128)(2,1)S(1)}, s32[]{:T(128)}, ...), condition=%wide.region_6.7_spmd, body=%wide.region_3.6_spmd.sunk | while | flops 274792448 | bytes 7092321 | solution.py:64
  194.5 0.7 fusion.62
  195.3 4.5 %convolution_convert_fusion.2 = bf16[1024,3072]{1,0:T(8,128)(2,1)} fusion(bf16[256,3072]{1,0:T(8,128)(2,1)S(1)} %bitcast.107, bf16[1024,128]{1,0:T(8,128)(2,1)S(1)} %collective-permute-done.1, bf16[1024,128]{1,0:T(8,128)(2,1)S(1)} %bitcast.113), kind=kOutput, calls=%fused_computation.32 | convolution fusion | flops 1614807040 | bytes 8388608 | tf_op jit(solution)/shard_map/dot_general | solution.py:106
  199.8 137.0 %reduce-scatter.2.cloned.1.call-done = bf16[32,3072]{1,0:T(8,128)(2,1)} async-done(((bf16[1024,3072]{1,0:T(8,128)(2,1)}), bf16[32,3072]{1,0:T(8,128)(2,1)}) %reduce-scatter.2.cloned.1.call-update) | async-done | bytes 196624 | tf_op jit(solution)/shard_map/reduce_scatter | solution.py:105
  336.9 1.7 fusion.38
  (54 shorter events, 12.0 us)
Async XLA Ops:
  6.5 188.7 %copy-start = (bf16[1,2,128,3072]{3,2,1,0:T(8,128)(2,1)S(1)}, bf16[1,2,128,3072]{3,2,1,0:T(8,128)(2,1)}, u32[]{:S(2)}) copy-start(bf16[1,2,128,3072]{3,2,1,0:T(8,128)(2,1)} %param.17) | copy-start | bytes 4718596
  6.6 160.3 %all-gather.2.cloned.1.call-start = ((), (), s32[]{:S(2)}) async-start(), calls=%async_computation.1 | async-start | bytes 6488064 | tf_op jit(solution)/shard_map/all_gather | solution.py:83
  11.5 325.4 %reduce-scatter.2.cloned.1.call-start = ((), (), s32[]{:S(2)}) async-start(), calls=%async_computation.2 | async-start | bytes 6488064 | tf_op jit(solution)/shard_map/reduce_scatter | solution.py:105
  15.6 4.8 %copy-start.3 = (f32[1,3,128]{2,0,1:T(1,128)S(1)}, f32[1,3,128]{2,0,1:T(1,128)}, u32[]{:S(2)}) copy-start(f32[1,3,128]{2,0,1:T(1,128)} %param.13) | copy-start | bytes 4612
  15.6 4.8 %copy-start.4 = (s32[2,1]{0,1:T(1,128)S(1)}, s32[2,1]{0,1:T(1,128)}, u32[]{:S(2)}) copy-start(s32[2,1]{0,1:T(1,128)} %param.14) | copy-start | bytes 28
  15.6 5.5 %copy-start.5 = (s32[2,1]{0,1:T(1,128)S(1)}, s32[2,1]{0,1:T(1,128)}, u32[]{:S(2)}) copy-start(s32[2,1]{0,1:T(1,128)} %param.15) | copy-start | bytes 28
  173.4 1.4 copy-start.2
  182.2 1.8 collective-permute-start
  189.3 5.9 %collective-permute-start.1 = (bf16[1024,128]{1,0:T(8,128)(2,1)S(1)}, bf16[1024,128]{1,0:T(8,128)(2,1)S(1)}, u32[]{:S(2)}, u32[]{:S(2)}) collective-permute-start(bf16[1024,128]{1,0:T(8,128)(2,1)S(1)} %bitcast.114), channel_id=1, source_target_pairs={{0,1},{1,0},{2,3},{3,2},{4,5},{5,4},{6,7},{7,6},{8,9},{9,8},{10,11... | collective-permute-start | bytes 786440 | tf_op jit(solution)/shard_map/ppermute | solution.py:16
  199.7 137.1 %copy-start.1 = (bf16[1,32,3072]{2,1,0:T(8,128)(2,1)S(1)}, bf16[1,32,3072]{2,1,0:T(8,128)(2,1)}, u32[]{:S(2)}) copy-start(bf16[1,32,3072]{2,1,0:T(8,128)(2,1)} %param.11) | copy-start | bytes 589828
Sparse Core Ops, SparseCore 0:
  11.6 155.1 all-gather.1
  199.9 136.8 reduce-scatter.1
where the time goes:
time: 346 us; the launch traced here: 345 us
  waiting for transfers between devices  280 us (81%)
  local copies, waits for them, and re-layouts  18.6 us (5%)
  other arithmetic  16.2 us (5%)
  matrix products  16 us (5%)
  between operations  13.6 us (4%)
    all_gather x1, waiting for transfers between devices, local(): row_piece = lax.all_gather(normed, 'tp', axis=0, tiled=True)  143 us
    reduce_scatter x1, waiting for transfers between devices, local(): lax.psum_scatter(jnp.dot(both_out, flat_out, preferred_element_type=jnp.f...  137 us
  transfers between devices with their start and end apart: 4, of which 2 were waited for; matrix products, arithmetic and copies ran while one was open for 6% of the time, Pallas kernels for 0%

commit v1 on v0

v1 whole, which is shorter than its diff:
```python
import functools
import math

import jax
import jax.numpy as jnp
import numpy as np
from jax import lax
from jax.experimental import pallas as pl
from jax.experimental.pallas import tpu as pltpu
from jax.sharding import PartitionSpec as P

MESH = pl.DeviceIdType.MESH
epsilon = 1e-06
rope_base = 10000.0
masked_score = -1e30
CHUNKS = 4


def kernel(
    n,
    h_ref,
    mod_ref,
    gain_ref,
    freq_ref,
    cnt_ref,
    off_ref,
    win_ref,
    wout_ref,
    out_ref,
    rows_all,
    raw,
    wide,
    w_in,
    w_out,
    acc,
    q_all,
    c_all,
    kv_own,
    kv_far,
    bias,
    both,
    part,
    rs_in,
    rs_out,
    w_sem,
    ag_send,
    ag_recv,
    kv_send,
    kv_recv,
    rs_send,
    rs_recv,
):
    half = n // 2
    me = lax.axis_index("tp")
    tower = lax.axis_index("tower")
    right = lax.rem(me + 1, n)
    left = lax.rem(me + n - 1, n)
    other = 1 - tower
    rows, width = h_ref.shape
    head = gain_ref.shape[-1]
    cols = width // CHUNKS
    tokens = n * rows
    score_scale = math.log2(math.e) / math.sqrt(head)

    win_copy = pltpu.make_async_copy(win_ref, raw, w_sem.at[0])
    wout_copy = pltpu.make_async_copy(wout_ref, w_out, w_sem.at[1])
    win_copy.start()
    wout_copy.start()

    barrier = pltpu.get_barrier_semaphore()
    for where in ({"tp": left}, {"tp": right}, {"tower": other}):
        pl.semaphore_signal(barrier, inc=1, device_id=where, device_id_type=MESH)

    def block(offset):
        return lax.rem(me + offset + 2 * n, n)

    def gather_copy(way, step, i):
        b = block(-step if way == 0 else step)
        return pltpu.make_async_remote_copy(
            src_ref=rows_all.at[b, i],
            dst_ref=rows_all.at[b, i],
            send_sem=ag_send.at[way, step, i],
            recv_sem=ag_recv.at[way, step, i],
            device_id={"tp": right if way == 0 else left},
            device_id_type=MESH,
        )

    def gather_arrival(way, step, i):
        b = block(-step if way == 0 else step)
        return pltpu.make_async_remote_copy(
            src_ref=rows_all.at[b, i],
            dst_ref=rows_all.at[b, i],
            send_sem=ag_send.at[way, step - 1, i],
            recv_sem=ag_recv.at[way, step - 1, i],
            device_id={"tp": right if way == 0 else left},
            device_id_type=MESH,
        )

    def kv_copy(b):
        return pltpu.make_async_remote_copy(
            src_ref=kv_own.at[b],
            dst_ref=kv_far.at[b],
            send_sem=kv_send.at[b],
            recv_sem=kv_recv.at[b],
            device_id={"tower": other},
            device_id_type=MESH,
        )

    def scatter_copy(way, step, i):
        return pltpu.make_async_remote_copy(
            src_ref=rs_out.at[way, step, i],
            dst_ref=rs_in.at[way, step, i],
            send_sem=rs_send.at[way, step, i],
            recv_sem=rs_recv.at[way, step, i],
            device_id={"tp": right if way == 0 else left},
            device_id_type=MESH,
        )

    states = h_ref[...].astype(jnp.float32)
    centre = states - jnp.mean(states, -1, keepdims=True)
    spread = jnp.mean(centre * centre, -1, keepdims=True)
    normed = centre * lax.rsqrt(spread + epsilon) * (1.0 + mod_ref[1:2, :]) + mod_ref[0:1, :]
    normed = normed.astype(jnp.bfloat16)
    for i in range(CHUNKS):
        rows_all[me, i] = normed[:, i * cols : (i + 1) * cols]

    key_index = lax.broadcasted_iota(jnp.int32, (1, tokens), 1)
    bias[0:1, :] = jnp.where(key_index < cnt_ref[tower, 0], 0.0, masked_score)
    bias[1:2, :] = jnp.where(key_index < cnt_ref[other, 0], 0.0, masked_score)

    pl.semaphore_wait(barrier, 3)
    for i in range(CHUNKS):
        gather_copy(0, 0, i).start()
        gather_copy(1, 0, i).start()

    win_copy.wait()
    fold = wide.shape[0] // 4

    def unfold(j, carry):
        wide[...] = raw[pl.ds(pl.multiple_of(j * 4 * fold, 4 * fold), 4 * fold), :].astype(jnp.float32)
        for c in range(4):
            w_in[pl.ds(pl.multiple_of(j * fold, fold), fold), c * head : (c + 1) * head] = wide[
                pl.ds(c, fold, stride=4), :
            ].astype(jnp.bfloat16)
        return carry

    lax.fori_loop(0, width // fold, unfold, 0)
    wout_copy.wait()

    lane = lax.broadcasted_iota(jnp.int32, (1, head), 1)
    is_even = lax.rem(lane, 2) == 0
    offset = off_ref[tower, 0]

    def row_positions(b):
        return offset + b * rows + lax.broadcasted_iota(jnp.int32, (rows, 1), 0)

    def project(i, blocks):
        picked = [rows_all[b, i] for b in blocks]
        lhs = picked[0] if len(picked) == 1 else jnp.concatenate(picked, 0)
        term = jnp.dot(lhs, w_in[i * cols : (i + 1) * cols, :], preferred_element_type=jnp.float32)
        if i == 0:
            acc[: lhs.shape[0], :] = term
        else:
            acc[: lhs.shape[0], :] += term

    def finish(blocks):
        count = len(blocks) * rows
        positions = [row_positions(b) for b in blocks]
        positions = positions[0] if len(blocks) == 1 else jnp.concatenate(positions, 0)
        angles = positions.astype(jnp.float32) * freq_ref[...]
        cosine = jnp.cos(angles)
        sine = jnp.sin(angles)
        sine = jnp.where(is_even, -sine, sine)

        def turned(c, g):
            x = acc[:count, c * head : (c + 1) * head]
            square = jnp.mean(x * x, -1, keepdims=True)
            x = x * lax.rsqrt(square + epsilon) * gain_ref[g : g + 1, :]
            swapped = jnp.where(is_even, pltpu.roll(x, head - 1, 1), pltpu.roll(x, 1, 1))
            return (x * cosine + swapped * sine).astype(jnp.bfloat16)

        queries = turned(0, 0)
        keys = turned(1, 1)
        values = acc[:count, 2 * head : 3 * head].astype(jnp.bfloat16)
        cross = turned(3, 2)
        for j, b in enumerate(blocks):
            span = slice(j * rows, (j + 1) * rows)
            q_all[b] = queries[span]
            kv_own[b, 0] = keys[span]
            kv_own[b, 1] = values[span]
            c_all[b] = cross[span]

    for i in range(CHUNKS):
        project(i, [me])
    finish([me])

    def gather_step(step, carry):
        before, after = block(-step), block(step)
        for i in range(CHUNKS):
            gather_arrival(0, step, i).wait_recv()
            if i < CHUNKS // 2:
                gather_copy(0, step, i).start()
            else:
                pl.when(step < half - 1)(lambda i=i: gather_copy(0, step, i).start())
            gather_arrival(1, step, i).wait_recv()
            if i < CHUNKS // 2:
                pl.when(step < half - 1)(lambda i=i: gather_copy(1, step, i).start())
            else:
                gather_copy(1, step, i).start()
            if i == 1:
                kv_copy(block(1 - step)).start()
                pl.when(step > 1)(lambda: kv_copy(block(step - 1)).start())
            project(i, [before, after])
        finish([before, after])
        return carry

    lax.fori_loop(1, half, gather_step, 0)
    kv_copy(block(1 - half)).start()
    kv_copy(block(half - 1)).start()
    last = block(half)
    for i in range(CHUNKS):
        gather_arrival(0 if i < CHUNKS // 2 else 1, half, i).wait_recv()
        project(i, [last])
    finish([last])

    def attend(queries, pairs, row):
        keys = pairs[:, 0].reshape(tokens, head)
        values = pairs[:, 1].reshape(tokens, head)
        scores = lax.dot_general(
            queries, keys, (((1,), (1,)), ((), ())), preferred_element_type=jnp.float32
        )
        scores = scores * score_scale + bias[row : row + 1, :]
        raised = jnp.exp2(scores - jnp.max(scores, -1, keepdims=True))
        total = jnp.sum(raised, -1, keepdims=True)
        summed = jnp.dot(raised.astype(jnp.bfloat16), values, preferred_element_type=jnp.float32)
        return (summed / total).astype(jnp.bfloat16)

    def attend_self(blocks):
        picked = [q_all[b] for b in blocks]
        lhs = picked[0] if len(picked) == 1 else jnp.concatenate(picked, 0)
        both[: lhs.shape[0], :head] = attend(lhs, kv_own, 0)

    def attend_cross(blocks):
        picked = [c_all[b] for b in blocks]
        lhs = picked[0] if len(picked) == 1 else jnp.concatenate(picked, 0)
        both[: lhs.shape[0], head:] = attend(lhs, kv_far, 1)

    def expand(count, i):
        return jnp.dot(
            both[:count, :], w_out[:, i * cols : (i + 1) * cols], preferred_element_type=jnp.float32
        )

    def partial_piece(slot, blocks, piece):
        if piece == 0:
            attend_self(blocks)
        elif piece == 1:
            attend_cross(blocks)
        else:
            for i in range(2 * (piece - 2), 2 * (piece - 1)):
                term = expand(2 * rows, i)
                part[slot, 0, i] = term[:rows]
                part[slot, 1, i] = term[rows:]

    attend_self([last])
    kv_copy(last).start()
    quiet = jnp.zeros((rows, cols), jnp.bfloat16)
    for i in range(CHUNKS):
        rs_in[1 if i < CHUNKS // 2 else 0, 0, i] = quiet

    def take_far(b, carry):
        kv_copy(b).wait_recv()
        return carry

    lax.fori_loop(0, n, take_far, 0)
    attend_cross([last])
    for i in range(CHUNKS):
        way = 0 if i < CHUNKS // 2 else 1
        rs_out[way, 0, i] = expand(rows, i).astype(jnp.bfloat16)
    for i in range(CHUNKS):
        scatter_copy(0 if i < CHUNKS // 2 else 1, 0, i).start()
    for piece in range(4):
        partial_piece(1, [block(half - 1), block(1 - half)], piece)

    def scatter_step(step, carry):
        slot = lax.rem(step, 2)
        following = [block(half - 1 - step), block(step + 1 - half)]
        for i in range(CHUNKS):
            for way in range(2):
                if (i < CHUNKS // 2) == (way == 0):
                    scatter_copy(way, step - 1, i).wait_recv()
                else:
                    pl.when(step > 1)(lambda way=way, i=i: scatter_copy(way, step - 1, i).wait_recv())
                running = rs_in[way, step - 1, i].astype(jnp.float32) + part[slot, way, i]
                rs_out[way, step, i] = running.astype(jnp.bfloat16)
                scatter_copy(way, step, i).start()
            partial_piece(1 - slot, following, i)
        return carry

    lax.fori_loop(1, half, scatter_step, 0)
    for i in range(CHUNKS):
        scatter_copy(0, half - 1, i).wait_recv()
        scatter_copy(1, half - 1, i).wait_recv()
        span = slice(i * cols, (i + 1) * cols)
        branch = part[half % 2, 0, i] + (
            rs_in[0, half - 1, i].astype(jnp.float32) + rs_in[1, half - 1, i].astype(jnp.float32)
        )
        out_ref[:, span] = (
            h_ref[:, span].astype(jnp.float32) + mod_ref[2:3, span] * branch
        ).astype(jnp.bfloat16)

    def settle(step, carry):
        for i in range(CHUNKS):
            for way in range(2):
                near = (i < CHUNKS // 2) == (way == 0)
                if near:
                    gather_copy(way, step, i).wait_send()
                    scatter_copy(way, step, i).wait_send()
                else:
                    pl.when(step < half - 1)(lambda way=way, i=i: gather_copy(way, step, i).wait_send())
                    pl.when(step > 0)(lambda way=way, i=i: scatter_copy(way, step, i).wait_send())
        return carry

    lax.fori_loop(0, half, settle, 0)

    def settle_far(b, carry):
        kv_copy(b).wait_send()
        return carry

    lax.fori_loop(0, n, settle_far, 0)


def local(n, hidden, modulation, qk_gains, counts, offsets, in_weights, out_weights):
    rows, width = hidden.shape[1:]
    head = in_weights.shape[-1]
    half = n // 2
    tokens = n * rows
    cols = width // CHUNKS
    frequency = np.repeat(
        np.exp(np.arange(head // 2, dtype=np.float64) * (-2.0 * math.log(rope_base) / head)), 2
    ).astype(np.float32)[None]
    vmem = pl.BlockSpec(memory_space=pltpu.VMEM)
    smem = pl.BlockSpec(memory_space=pltpu.SMEM)
    anywhere = pl.BlockSpec(memory_space=pl.ANY)
    updated = pl.pallas_call(
        functools.partial(kernel, n),
        out_shape=jax.ShapeDtypeStruct((rows, width), jnp.bfloat16),
        in_specs=[vmem, vmem, vmem, vmem, smem, smem, anywhere, anywhere],
        out_specs=vmem,
        scratch_shapes=[
            pltpu.VMEM((n, CHUNKS, rows, cols), jnp.bfloat16),
            pltpu.VMEM((width * 4, head), jnp.bfloat16),
            pltpu.VMEM((4 * 128, head), jnp.float32),
            pltpu.VMEM((width, 4 * head), jnp.bfloat16),
            pltpu.VMEM((2 * head, width), jnp.bfloat16),
            pltpu.VMEM((2 * rows, 4 * head), jnp.float32),
            pltpu.VMEM((n, rows, head), jnp.bfloat16),
            pltpu.VMEM((n, rows, head), jnp.bfloat16),
            pltpu.VMEM((n, 2, rows, head), jnp.bfloat16),
            pltpu.VMEM((n, 2, rows, head), jnp.bfloat16),
            pltpu.VMEM((2, tokens), jnp.float32),
            pltpu.VMEM((2 * rows, 2 * head), jnp.bfloat16),
            pltpu.VMEM((2, 2, CHUNKS, rows, cols), jnp.float32),
            pltpu.VMEM((2, half, CHUNKS, rows, cols), jnp.bfloat16),
            pltpu.VMEM((2, half, CHUNKS, rows, cols), jnp.bfloat16),
            pltpu.SemaphoreType.DMA((2,)),
            pltpu.SemaphoreType.DMA((2, half, CHUNKS)),
            pltpu.SemaphoreType.DMA((2, half, CHUNKS)),
            pltpu.SemaphoreType.DMA((n,)),
            pltpu.SemaphoreType.DMA((n,)),
            pltpu.SemaphoreType.DMA((2, half, CHUNKS)),
            pltpu.SemaphoreType.DMA((2, half, CHUNKS)),
        ],
        compiler_params=pltpu.CompilerParams(
            collective_id=0, has_side_effects=True, vmem_limit_bytes=56 * 1024 * 1024
        ),
    )(
        hidden[0],
        modulation[0],
        qk_gains[0].reshape(3, head),
        jnp.asarray(frequency),
        counts,
        offsets,
        in_weights.reshape(4 * width, head),
        out_weights.reshape(2 * head, width),
    )
    return updated[None]


def solution(mesh):
    return jax.shard_map(
        functools.partial(local, mesh.shape["tp"]),
        mesh=mesh,
        in_specs=(
            P("tower", ("grp", "tp"), None),
            P("tower", None, None),
            P("tower", None, "tp"),
            P(None, "grp"),
            P(None, "grp"),
            P("tower", None, None, "tp"),
            P("tower", None, "tp", None),
        ),
        out_specs=P("tower", ("grp", "tp"), None),
        check_vma=False,
    )
```

time: 346 us -> 179 us (0.52)
  waiting for transfers between devices: 280 us -> 0 us
  Pallas kernels: 0 us -> 171 us
  other arithmetic: 16.2 us -> 0 us
  matrix products: 16 us -> 0 us
  between operations: 13.6 us -> 0.01 us
  local copies, waits for them, and re-layouts: 18.6 us -> 6.81 us
    pallas_call x0 -> x1, Pallas kernels: none -> 171 us  [local(): pl.pallas_call(functools.partial(kernel, n), out_shape=jax.ShapeDtypeStru...]
    all_gather x1 -> x0, waiting for transfers between devices: 143 us -> none  [local(): row_piece = lax.all_gather(normed, 'tp', axis=0, tiled=True)]
    reduce_scatter x1 -> x0, waiting for transfers between devices: 137 us -> none  [local(): lax.psum_scatter(jnp.dot(both_out, flat_out, preferred_element_type=jnp.f...]
    dot_general x10 -> x0, matrix products: 16 us -> none  [the longest x1 6.51 us: local(): jnp.dot(row_piece, flat_weights, preferred_element_type=jnp.float32)]
    dot_general x1 -> x0, local copies, waits for them, and re-layouts: 4.77 us -> none  [local(): jnp.dot(row_piece, flat_weights, preferred_element_type=jnp.float32)]
    reduce_sum x7 -> x0, other arithmetic: 4.73 us -> none  [the longest x4 2.35 us: attend(): jnp.sum(raised, -1, keepdims=True)]
    slice x5 -> x0, local copies, waits for them, and re-layouts: 4.44 us -> none  [the longest x1 2.16 us: rotate(): odd_part = columns[..., 1::2]]
  transfers between devices with their start and end apart: 4 -> 0, of which waited for: 2 -> 0; matrix products, arithmetic and copies ran while one was open for 6% -> 0% of each run, Pallas kernels for 0% -> 0%
where the time goes in v1:
time: 179 us; the launch traced here: 178 us
  Pallas kernels  171 us (96%)
  local copies, waits for them, and re-layouts  6.81 us (4%)
    pallas_call x1, Pallas kernels, local(): pl.pallas_call(functools.partial(kernel, n), out_shape=jax.ShapeDtypeStru...  171 us
    unnamed x5, local copies, waits for them, and re-layouts  6.81 us

profile of v1, /device:TPU:38, one launch (start us, length us, event | category | flops | bytes accessed | tf_op | source)
XLA Modules:
  0.0 177.7 jit_solution(2364493683217666352)
XLA Ops:
  0.0 1.3 copy.9.cnt_ref
  1.3 1.3 copy.10.off_ref
  2.5 1.3 copy.16
  3.8 1.4 copy.15
  5.2 170.9 %shard_map.82 = bf16[32,3072]{1,0:T(8,128)(2,1)} custom-call(bf16[32,3072]{1,0:T(8,128)(2,1)} %bitcast.14, f32[3,3072]{1,0:T(4,128)} %bitcast.13, f32[3,128]{1,0:T(4,128)} %bitcast.15, f32[1,128]{1,0:T(1,128)} %constant.2.clone.freq_ref, s32[2,1]{1,0:T(2,128)} %copy.9.cnt_ref, s32[2,1]{1,0:T(2,128)} %copy.10.off_ref, bf16[12288,128]{1,0:T(8,128)(2,1)} %bitcast.10, ...), custom_call_target="tpu_custom_call" | custom-call | tf_op jit(solution)/shard_map/pallas_call | solution.py:344
  176.1 1.6 copy.18

commit v2 on v1

v2 whole, which is shorter than its diff:
```python
import functools
import math

import jax
import jax.numpy as jnp
import numpy as np
from jax import lax
from jax.experimental import pallas as pl
from jax.experimental.pallas import tpu as pltpu
from jax.sharding import PartitionSpec as P

MESH = pl.DeviceIdType.MESH
epsilon = 1e-06
rope_base = 10000.0
masked_score = -1e30
CHUNKS = 4


def kernel(
    n,
    h_hbm,
    mod_hbm,
    gain_hbm,
    freq_hbm,
    cnt_hbm,
    off_hbm,
    win_hbm,
    wout_hbm,
    out_ref,
    h_ref,
    mod_ref,
    gain_ref,
    freq_ref,
    cnt_ref,
    off_ref,
    rows_all,
    raw,
    wide,
    w_in,
    w_out,
    acc,
    q_all,
    c_all,
    kv_own,
    kv_far,
    bias,
    trig,
    both,
    part,
    rs_in,
    rs_out,
    w_sem,
    out_sem,
    ag_recv,
    kv_recv,
    rs_recv,
):
    half = n // 2
    me = lax.axis_index("tp")
    tower = lax.axis_index("tower")
    right = lax.rem(me + 1, n)
    left = lax.rem(me + n - 1, n)
    other = 1 - tower
    depth = rs_recv.shape[1]
    rows, width = h_ref.shape
    head = gain_ref.shape[-1]
    cols = width // CHUNKS
    tokens = n * rows
    score_scale = math.log2(math.e) / math.sqrt(head)

    loads = [
        pltpu.make_async_copy(source, target, w_sem.at[j])
        for j, (source, target) in enumerate(
            (
                (h_hbm, h_ref),
                (mod_hbm, mod_ref),
                (win_hbm, raw),
                (cnt_hbm, cnt_ref),
                (off_hbm, off_ref),
                (gain_hbm, gain_ref),
                (freq_hbm, freq_ref),
                (wout_hbm, w_out),
            )
        )
    ]
    h_copy, mod_copy, win_copy, cnt_copy, off_copy, gain_copy, freq_copy, wout_copy = loads
    for load in loads:
        load.start()

    barrier = pltpu.get_barrier_semaphore()
    for where in ({"tp": left}, {"tp": right}, {"tower": other}):
        pl.semaphore_signal(barrier, inc=1, device_id=where, device_id_type=MESH)

    def block(offset):
        return lax.rem(me + offset + 2 * n, n)

    def gather_copy(way, step, i):
        piece = block(-step if way == 0 else step) * CHUNKS + i
        return pltpu.make_async_remote_copy(
            src_ref=rows_all.at[piece],
            dst_ref=rows_all.at[piece],
            send_sem=out_sem.at[0],
            recv_sem=ag_recv.at[way, lax.rem(step, depth), i],
            device_id={"tp": right if way == 0 else left},
            device_id_type=MESH,
        )

    def gather_arrival(way, step, i):
        return gather_copy(way, step - 1, i)

    def kv_copy(b):
        return pltpu.make_async_remote_copy(
            src_ref=kv_own.at[b],
            dst_ref=kv_far.at[b],
            send_sem=out_sem.at[1],
            recv_sem=kv_recv,
            device_id={"tower": other},
            device_id_type=MESH,
        )

    def scatter_copy(way, step, i):
        piece = (way * half + step) * CHUNKS + i
        return pltpu.make_async_remote_copy(
            src_ref=rs_out.at[piece],
            dst_ref=rs_in.at[piece],
            send_sem=out_sem.at[2],
            recv_sem=rs_recv.at[way, lax.rem(step, depth), i],
            device_id={"tp": right if way == 0 else left},
            device_id_type=MESH,
        )

    def all_sent(ref, count, sem):
        return pltpu.make_async_remote_copy(
            src_ref=ref.at[pl.ds(0, count)],
            dst_ref=ref.at[pl.ds(0, count)],
            send_sem=sem,
            recv_sem=kv_recv,
            device_id={"tower": other},
            device_id_type=MESH,
        )

    h_copy.wait()
    mod_copy.wait()
    states = h_ref[...].astype(jnp.float32)
    centre = states - jnp.mean(states, -1, keepdims=True)
    spread = jnp.mean(centre * centre, -1, keepdims=True)
    normed = centre * lax.rsqrt(spread + epsilon) * (1.0 + mod_ref[1]) + mod_ref[0]
    normed = normed.astype(jnp.bfloat16)
    for i in range(CHUNKS):
        rows_all[me * CHUNKS + i] = normed[:, i * cols : (i + 1) * cols]

    pl.semaphore_wait(barrier, 3)
    for i in range(CHUNKS):
        gather_copy(0, 0, i).start()
        gather_copy(1, 0, i).start()

    cnt_copy.wait()
    key_index = lax.broadcasted_iota(jnp.int32, (1, tokens), 1)
    bias[0:1, :] = jnp.where(key_index < cnt_ref[0, tower], 0.0, masked_score)
    bias[1:2, :] = jnp.where(key_index < cnt_ref[0, other], 0.0, masked_score)

    win_copy.wait()
    fold = wide.shape[0] // 4

    def unfold(j, carry):
        wide[...] = raw[pl.ds(pl.multiple_of(j * 4 * fold, 4 * fold), 4 * fold), :].astype(jnp.float32)
        for c in range(4):
            w_in[pl.ds(pl.multiple_of(j * fold, fold), fold), c * head : (c + 1) * head] = wide[
                pl.ds(c, fold, stride=4), :
            ].astype(jnp.bfloat16)
        return carry

    lax.fori_loop(0, width // fold, unfold, 0)
    for load in (off_copy, gain_copy, freq_copy, wout_copy):
        load.wait()

    lane = lax.broadcasted_iota(jnp.int32, (1, head), 1)
    is_even = lax.rem(lane, 2) == 0
    offset = off_ref[0, tower]

    def row_positions(b):
        return offset + b * rows + lax.broadcasted_iota(jnp.int32, (rows, 1), 0)

    def project(i, blocks):
        picked = [rows_all[b * CHUNKS + i] for b in blocks]
        lhs = picked[0] if len(picked) == 1 else jnp.concatenate(picked, 0)
        term = jnp.dot(lhs, w_in[i * cols : (i + 1) * cols, :], preferred_element_type=jnp.float32)
        if i == 0:
            acc[: lhs.shape[0], :] = term
        else:
            acc[: lhs.shape[0], :] += term

    def prepare_turn(blocks):
        for j, b in enumerate(blocks):
            angles = row_positions(b).astype(jnp.float32) * freq_ref[...]
            sine = jnp.sin(angles)
            trig[0, j * rows : (j + 1) * rows] = jnp.cos(angles)
            trig[1, j * rows : (j + 1) * rows] = jnp.where(is_even, -sine, sine)

    def finish(blocks):
        count = len(blocks) * rows
        cosine = trig[0, :count]
        sine = trig[1, :count]

        def turned(c, g):
            x = acc[:count, c * head : (c + 1) * head]
            square = jnp.mean(x * x, -1, keepdims=True)
            x = x * lax.rsqrt(square + epsilon) * gain_ref[g]
            swapped = jnp.where(is_even, pltpu.roll(x, head - 1, 1), pltpu.roll(x, 1, 1))
            return (x * cosine + swapped * sine).astype(jnp.bfloat16)

        keys = turned(1, 1)
        values = acc[:count, 2 * head : 3 * head].astype(jnp.bfloat16)
        for j, b in enumerate(blocks):
            span = slice(j * rows, (j + 1) * rows)
            kv_own[b, 0] = keys[span]
            kv_own[b, 1] = values[span]
        queries = turned(0, 0)
        cross = turned(3, 2)
        for j, b in enumerate(blocks):
            span = slice(j * rows, (j + 1) * rows)
            q_all[b] = queries[span]
            c_all[b] = cross[span]

    for i in range(CHUNKS):
        project(i, [me])
    prepare_turn([me])
    finish([me])

    def gather_step(step, carry):
        before, after = block(-step), block(step)
        prepare_turn([before, after])
        for i in range(CHUNKS):
            gather_arrival(0, step, i).wait_recv()
            if i < CHUNKS // 2:
                gather_copy(0, step, i).start()
            else:
                pl.when(step < half - 1)(lambda i=i: gather_copy(0, step, i).start())
            gather_arrival(1, step, i).wait_recv()
            if i < CHUNKS // 2:
                pl.when(step < half - 1)(lambda i=i: gather_copy(1, step, i).start())
            else:
                gather_copy(1, step, i).start()
            if i == 1:
                kv_copy(block(1 - step)).start()
                pl.when(step > 1)(lambda: kv_copy(block(step - 1)).start())
            project(i, [before, after])
        finish([before, after])
        return carry

    lax.fori_loop(1, half, gather_step, 0)
    kv_copy(block(1 - half)).start()
    kv_copy(block(half - 1)).start()
    last = block(half)
    prepare_turn([last])
    quiet = jnp.zeros((rows, cols), jnp.bfloat16)
    for i in range(CHUNKS):
        rs_in[(half if i < CHUNKS // 2 else 0) * CHUNKS + i] = quiet
    for i in range(CHUNKS):
        gather_arrival(0 if i < CHUNKS // 2 else 1, half, i).wait_recv()
        project(i, [last])
    finish([last])
    kv_copy(last).start()

    def attend(queries, pairs, row):
        keys = pairs[:, 0].reshape(tokens, head)
        values = pairs[:, 1].reshape(tokens, head)
        scores = lax.dot_general(
            queries, keys, (((1,), (1,)), ((), ())), preferred_element_type=jnp.float32
        )
        scores = scores * score_scale + bias[row : row + 1, :]
        raised = jnp.exp2(scores - jnp.max(scores, -1, keepdims=True))
        total = jnp.sum(raised, -1, keepdims=True)
        summed = jnp.dot(raised.astype(jnp.bfloat16), values, preferred_element_type=jnp.float32)
        return (summed / total).astype(jnp.bfloat16)

    def attend_self(blocks):
        picked = [q_all[b] for b in blocks]
        lhs = picked[0] if len(picked) == 1 else jnp.concatenate(picked, 0)
        both[: lhs.shape[0], :head] = attend(lhs, kv_own, 0)

    def attend_cross(blocks):
        picked = [c_all[b] for b in blocks]
        lhs = picked[0] if len(picked) == 1 else jnp.concatenate(picked, 0)
        both[: lhs.shape[0], head:] = attend(lhs, kv_far, 1)

    def expand(count, i):
        return jnp.dot(
            both[:count, :], w_out[:, i * cols : (i + 1) * cols], preferred_element_type=jnp.float32
        )

    def partial_piece(slot, blocks, piece):
        if piece == 0:
            attend_self(blocks)
        elif piece == 1:
            attend_cross(blocks)
        else:
            for i in range(2 * (piece - 2), 2 * (piece - 1)):
                term = expand(2 * rows, i)
                part[slot, 0, i] = term[:rows]
                part[slot, 1, i] = term[rows:]

    attend_self([last])
    pltpu.make_async_copy(kv_far, kv_far, kv_recv).wait()
    attend_cross([last])
    for i in (0, 2, 1, 3):
        way = 0 if i < CHUNKS // 2 else 1
        rs_out[way * half * CHUNKS + i] = expand(rows, i).astype(jnp.bfloat16)
        scatter_copy(way, 0, i).start()
    for piece in range(4):
        partial_piece(1, [block(half - 1), block(1 - half)], piece)

    def scatter_step(step, carry):
        slot = lax.rem(step, 2)
        following = [block(half - 1 - step), block(step + 1 - half)]
        for i in range(CHUNKS):
            for way in range(2):
                if (i < CHUNKS // 2) == (way == 0):
                    scatter_copy(way, step - 1, i).wait_recv()
                else:
                    pl.when(step > 1)(lambda way=way, i=i: scatter_copy(way, step - 1, i).wait_recv())
                running = rs_in[(way * half + step - 1) * CHUNKS + i].astype(jnp.float32) + part[slot, way, i]
                rs_out[(way * half + step) * CHUNKS + i] = running.astype(jnp.bfloat16)
                scatter_copy(way, step, i).start()
            partial_piece(1 - slot, following, i)
        return carry

    lax.fori_loop(1, half, scatter_step, 0)
    for i in range(CHUNKS):
        scatter_copy(0, half - 1, i).wait_recv()
        scatter_copy(1, half - 1, i).wait_recv()
        span = slice(i * cols, (i + 1) * cols)
        branch = part[half % 2, 0, i] + (
            rs_in[(half - 1) * CHUNKS + i].astype(jnp.float32)
            + rs_in[(2 * half - 1) * CHUNKS + i].astype(jnp.float32)
        )
        out_ref[:, span] = (
            h_ref[:, span].astype(jnp.float32) + mod_ref[2, :, span] * branch
        ).astype(jnp.bfloat16)

    moved = (2 * half - 1) * CHUNKS
    all_sent(rows_all, moved, out_sem.at[0]).wait_send()
    all_sent(kv_own, n, out_sem.at[1]).wait_send()
    all_sent(rs_out, moved, out_sem.at[2]).wait_send()


def local(n, hidden, modulation, qk_gains, counts, offsets, in_weights, out_weights):
    rows, width = hidden.shape[1:]
    head = in_weights.shape[-1]
    half = n // 2
    tokens = n * rows
    cols = width // CHUNKS
    frequency = np.repeat(
        np.exp(np.arange(head // 2, dtype=np.float64) * (-2.0 * math.log(rope_base) / head)), 2
    ).astype(np.float32)[None]
    vmem = pl.BlockSpec(memory_space=pltpu.VMEM)
    anywhere = pl.BlockSpec(memory_space=pl.ANY)
    updated = pl.pallas_call(
        functools.partial(kernel, n),
        out_shape=jax.ShapeDtypeStruct((rows, width), jnp.bfloat16),
        in_specs=[anywhere] * 8,
        out_specs=vmem,
        scratch_shapes=[
            pltpu.VMEM((rows, width), jnp.bfloat16),
            pltpu.VMEM((3, 1, width), jnp.float32),
            pltpu.VMEM((3, 1, head), jnp.float32),
            pltpu.VMEM((1, head), jnp.float32),
            pltpu.SMEM((1, 2), jnp.int32),
            pltpu.SMEM((1, 2), jnp.int32),
            pltpu.VMEM((n * CHUNKS, rows, cols), jnp.bfloat16),
            pltpu.VMEM((width * 4, head), jnp.bfloat16),
            pltpu.VMEM((4 * 128, head), jnp.float32),
            pltpu.VMEM((width, 4 * head), jnp.bfloat16),
            pltpu.VMEM((2 * head, width), jnp.bfloat16),
            pltpu.VMEM((2 * rows, 4 * head), jnp.float32),
            pltpu.VMEM((n, rows, head), jnp.bfloat16),
            pltpu.VMEM((n, rows, head), jnp.bfloat16),
            pltpu.VMEM((n, 2, rows, head), jnp.bfloat16),
            pltpu.VMEM((n, 2, rows, head), jnp.bfloat16),
            pltpu.VMEM((2, tokens), jnp.float32),
            pltpu.VMEM((2, 2 * rows, head), jnp.float32),
            pltpu.VMEM((2 * rows, 2 * head), jnp.bfloat16),
            pltpu.VMEM((2, 2, CHUNKS, rows, cols), jnp.float32),
            pltpu.VMEM((2 * half * CHUNKS, rows, cols), jnp.bfloat16),
            pltpu.VMEM((2 * half * CHUNKS, rows, cols), jnp.bfloat16),
            pltpu.SemaphoreType.DMA((8,)),
            pltpu.SemaphoreType.DMA((3,)),
            pltpu.SemaphoreType.DMA((2, 4, CHUNKS)),
            pltpu.SemaphoreType.DMA,
            pltpu.SemaphoreType.DMA((2, 4, CHUNKS)),
        ],
        compiler_params=pltpu.CompilerParams(
            collective_id=0, has_side_effects=True, vmem_limit_bytes=56 * 1024 * 1024
        ),
    )(
        hidden[0],
        jnp.transpose(modulation, (1, 0, 2)),
        jnp.transpose(qk_gains, (1, 0, 2)),
        jnp.asarray(frequency),
        counts.T,
        offsets.T,
        in_weights.reshape(4 * width, head),
        out_weights.reshape(2 * head, width),
    )
    return updated[None]


def solution(mesh):
    return jax.shard_map(
        functools.partial(local, mesh.shape["tp"]),
        mesh=mesh,
        in_specs=(
            P("tower", ("grp", "tp"), None),
            P("tower", None, None),
            P("tower", None, "tp"),
            P(None, "grp"),
            P(None, "grp"),
            P("tower", None, None, "tp"),
            P("tower", None, "tp", None),
        ),
        out_specs=P("tower", ("grp", "tp"), None),
        check_vma=False,
    )
```

time: 179 us -> 167 us (0.933)
  Pallas kernels: 171 us -> 165 us
  local copies, waits for them, and re-layouts: 6.81 us -> 1.62 us
    pallas_call x1, Pallas kernels: 171 us -> 165 us  [local(): pl.pallas_call(functools.partial(kernel, n), out_shape=jax.ShapeDtypeStru...]
    unnamed x5 -> x1, local copies, waits for them, and re-layouts: 6.81 us -> 1.62 us
where the time goes in v2:
time: 167 us; the launch traced here: 166 us
  Pallas kernels  165 us (99%)
    pallas_call x1, Pallas kernels, local(): pl.pallas_call(functools.partial(kernel, n), out_shape=jax.ShapeDtypeStru...  165 us

profile of v2, /device:TPU:38, one launch (start us, length us, event | category | flops | bytes accessed | tf_op | source)
XLA Modules:
  0.0 166.4 jit_solution(9001613452811690468)
XLA Ops:
  0.0 164.8 %shard_map.82 = bf16[32,3072]{1,0:T(8,128)(2,1)} custom-call(bf16[32,3072]{1,0:T(8,128)(2,1)} %bitcast.11, f32[3,1,3072]{2,1,0:T(1,128)} %bitcast.12, f32[3,1,128]{2,1,0:T(1,128)} %bitcast.13, f32[1,128]{1,0:T(1,128)} %constant.2.clone.freq_hbm, s32[1,2]{1,0:T(1,128)} %bitcast.14, s32[1,2]{1,0:T(1,128)} %bitcast.15, bf16[12288,128]{1,0:T(8,128)(2,1)} %bitcast.8, ...), custom_call_target="tpu_custom_call" | custom-call | tf_op jit(solution)/shard_map/pallas_call | solution.py:358
  164.8 1.6 copy.10

commit v3 on v2

--- a/solution.py
+++ b/solution.py
@@ -129,6 +129,12 @@
             device_id_type=MESH,
         )
 
+    def gather_chunk(way, slot):
+        return slot if way == 0 else (slot + CHUNKS // 2) % CHUNKS
+
+    def scatter_chunk(way, slot):
+        return gather_chunk(1 - way, slot)
+
     def all_sent(ref, count, sem):
         return pltpu.make_async_remote_copy(
             src_ref=ref.at[pl.ds(0, count)],
@@ -150,9 +156,9 @@
         rows_all[me * CHUNKS + i] = normed[:, i * cols : (i + 1) * cols]
 
     pl.semaphore_wait(barrier, 3)
-    for i in range(CHUNKS):
-        gather_copy(0, 0, i).start()
-        gather_copy(1, 0, i).start()
+    for slot in range(CHUNKS):
+        for way in range(2):
+            gather_copy(way, 0, gather_chunk(way, slot)).start()
 
     cnt_copy.wait()
     key_index = lax.broadcasted_iota(jnp.int32, (1, tokens), 1)
@@ -181,11 +187,11 @@
     def row_positions(b):
         return offset + b * rows + lax.broadcasted_iota(jnp.int32, (rows, 1), 0)
 
-    def project(i, blocks):
+    def project(i, blocks, first):
         picked = [rows_all[b * CHUNKS + i] for b in blocks]
         lhs = picked[0] if len(picked) == 1 else jnp.concatenate(picked, 0)
         term = jnp.dot(lhs, w_in[i * cols : (i + 1) * cols, :], preferred_element_type=jnp.float32)
-        if i == 0:
+        if first:
             acc[: lhs.shape[0], :] = term
         else:
             acc[: lhs.shape[0], :] += term
@@ -197,7 +203,7 @@
             trig[0, j * rows : (j + 1) * rows] = jnp.cos(angles)
             trig[1, j * rows : (j + 1) * rows] = jnp.where(is_even, -sine, sine)
 
-    def finish(blocks):
+    def finish(blocks, send=False):
         count = len(blocks) * rows
         cosine = trig[0, :count]
         sine = trig[1, :count]
@@ -215,6 +221,8 @@
             span = slice(j * rows, (j + 1) * rows)
             kv_own[b, 0] = keys[span]
             kv_own[b, 1] = values[span]
+            if send:
+                kv_copy(b).start()
         queries = turned(0, 0)
         cross = turned(3, 2)
         for j, b in enumerate(blocks):
@@ -223,28 +231,27 @@
             c_all[b] = cross[span]
 
     for i in range(CHUNKS):
-        project(i, [me])
+        project(i, [me], i == 0)
     prepare_turn([me])
     finish([me])
 
     def gather_step(step, carry):
         before, after = block(-step), block(step)
         prepare_turn([before, after])
-        for i in range(CHUNKS):
-            gather_arrival(0, step, i).wait_recv()
-            if i < CHUNKS // 2:
-                gather_copy(0, step, i).start()
-            else:
-                pl.when(step < half - 1)(lambda i=i: gather_copy(0, step, i).start())
-            gather_arrival(1, step, i).wait_recv()
-            if i < CHUNKS // 2:
-                pl.when(step < half - 1)(lambda i=i: gather_copy(1, step, i).start())
-            else:
-                gather_copy(1, step, i).start()
-            if i == 1:
+        for slot in range(CHUNKS):
+            for way in range(2):
+                i = gather_chunk(way, slot)
+                gather_arrival(way, step, i).wait_recv()
+                if slot < CHUNKS // 2:
+                    gather_copy(way, step, i).start()
+                else:
+                    pl.when(step < half - 1)(lambda way=way, i=i: gather_copy(way, step, i).start())
+            if slot == 0:
                 kv_copy(block(1 - step)).start()
                 pl.when(step > 1)(lambda: kv_copy(block(step - 1)).start())
-            project(i, [before, after])
+            if slot >= CHUNKS // 2:
+                project(gather_chunk(0, slot), [before, after], slot == CHUNKS // 2)
+                project(gather_chunk(1, slot), [before, after], False)
         finish([before, after])
         return carry
 
@@ -256,11 +263,12 @@
     quiet = jnp.zeros((rows, cols), jnp.bfloat16)
     for i in range(CHUNKS):
         rs_in[(half if i < CHUNKS // 2 else 0) * CHUNKS + i] = quiet
-    for i in range(CHUNKS):
-        gather_arrival(0 if i < CHUNKS // 2 else 1, half, i).wait_recv()
-        project(i, [last])
-    finish([last])
-    kv_copy(last).start()
+    for slot in range(CHUNKS // 2):
+        for way in range(2):
+            i = gather_chunk(way, slot)
+            gather_arrival(way, half, i).wait_recv()
+            project(i, [last], slot == 0 and way == 0)
+    finish([last], True)
 
     def attend(queries, pairs, row):
         keys = pairs[:, 0].reshape(tokens, head)
@@ -289,7 +297,7 @@
             both[:count, :], w_out[:, i * cols : (i + 1) * cols], preferred_element_type=jnp.float32
         )
 
-    def partial_piece(slot, blocks, piece):
+    def partial_piece(turn, blocks, piece):
         if piece == 0:
             attend_self(blocks)
         elif piece == 1:
@@ -297,8 +305,8 @@
         else:
             for i in range(2 * (piece - 2), 2 * (piece - 1)):
                 term = expand(2 * rows, i)
-                part[slot, 0, i] = term[:rows]
-                part[slot, 1, i] = term[rows:]
+                part[turn, 0, i] = term[:rows]
+                part[turn, 1, i] = term[rows:]
 
     attend_self([last])
     pltpu.make_async_copy(kv_far, kv_far, kv_recv).wait()
@@ -311,22 +319,23 @@
         partial_piece(1, [block(half - 1), block(1 - half)], piece)
 
     def scatter_step(step, carry):
-        slot = lax.rem(step, 2)
+        turn = lax.rem(step, 2)
         following = [block(half - 1 - step), block(step + 1 - half)]
-        for i in range(CHUNKS):
+        for slot in range(CHUNKS):
             for way in range(2):
-                if (i < CHUNKS // 2) == (way == 0):
+                i = scatter_chunk(way, slot)
+                if slot >= CHUNKS // 2:
                     scatter_copy(way, step - 1, i).wait_recv()
                 else:
                     pl.when(step > 1)(lambda way=way, i=i: scatter_copy(way, step - 1, i).wait_recv())
-                running = rs_in[(way * half + step - 1) * CHUNKS + i].astype(jnp.float32) + part[slot, way, i]
+                running = rs_in[(way * half + step - 1) * CHUNKS + i].astype(jnp.float32) + part[turn, way, i]
                 rs_out[(way * half + step) * CHUNKS + i] = running.astype(jnp.bfloat16)
                 scatter_copy(way, step, i).start()
-            partial_piece(1 - slot, following, i)
+            partial_piece(1 - turn, following, slot)
         return carry
 
     lax.fori_loop(1, half, scatter_step, 0)
-    for i in range(CHUNKS):
+    for i in (0, 2, 1, 3):
         scatter_copy(0, half - 1, i).wait_recv()
         scatter_copy(1, half - 1, i).wait_recv()
         span = slice(i * cols, (i + 1) * cols)
@@ -357,7 +366,7 @@
     anywhere = pl.BlockSpec(memory_space=pl.ANY)
     updated = pl.pallas_call(
         functools.partial(kernel, n),
-        out_shape=jax.ShapeDtypeStruct((rows, width), jnp.bfloat16),
+        out_shape=pltpu.VMEM((rows, width), jnp.bfloat16),
         in_specs=[anywhere] * 8,
         out_specs=vmem,
         scratch_shapes=[

time: 167 us -> 163 us (0.976)
  Pallas kernels: 165 us -> 161 us
    pallas_call x1, Pallas kernels: 165 us -> 161 us  [local(): pl.pallas_call(functools.partial(kernel, n), out_shape=pltpu.VMEM((rows,...]
where the time goes in v3:
time: 163 us; the launch traced here: 162 us
  Pallas kernels  161 us (99%)
    pallas_call x1, Pallas kernels, local(): pl.pallas_call(functools.partial(kernel, n), out_shape=pltpu.VMEM((rows,...  161 us

profile of v3, /device:TPU:38, one launch (start us, length us, event | category | flops | bytes accessed | tf_op | source)
XLA Modules:
  0.0 162.0 jit_solution(9616398756626550391)
XLA Ops:
  0.0 161.3 %shard_map.82 = bf16[32,3072]{1,0:T(8,128)(2,1)S(1)} custom-call(bf16[32,3072]{1,0:T(8,128)(2,1)} %bitcast.11, f32[3,1,3072]{2,1,0:T(1,128)} %bitcast.12, f32[3,1,128]{2,1,0:T(1,128)} %bitcast.13, f32[1,128]{1,0:T(1,128)} %constant.2.clone.freq_hbm, s32[1,2]{1,0:T(1,128)} %bitcast.14, s32[1,2]{1,0:T(1,128)} %bitcast.15, bf16[12288,128]{1,0:T(8,128)(2,1)} %bitcast.9, ...), custom_call_target="tpu_custom_call" | custom-call | tf_op jit(solution)/shard_map/pallas_call | solution.py:367
  161.4 0.7 copy.10

commit v4 on v3

--- a/solution.py
+++ b/solution.py
@@ -51,9 +51,8 @@
     rs_out,
     w_sem,
     out_sem,
-    ag_recv,
+    recv,
     kv_recv,
-    rs_recv,
 ):
     half = n // 2
     me = lax.axis_index("tp")
@@ -61,7 +60,7 @@
     right = lax.rem(me + 1, n)
     left = lax.rem(me + n - 1, n)
     other = 1 - tower
-    depth = rs_recv.shape[1]
+    depth = recv.shape[1]
     rows, width = h_ref.shape
     head = gain_ref.shape[-1]
     cols = width // CHUNKS
@@ -100,7 +99,7 @@
             src_ref=rows_all.at[piece],
             dst_ref=rows_all.at[piece],
             send_sem=out_sem.at[0],
-            recv_sem=ag_recv.at[way, lax.rem(step, depth), i],
+            recv_sem=recv.at[way, lax.rem(step, depth), i],
             device_id={"tp": right if way == 0 else left},
             device_id_type=MESH,
         )
@@ -124,7 +123,7 @@
             src_ref=rs_out.at[piece],
             dst_ref=rs_in.at[piece],
             send_sem=out_sem.at[2],
-            recv_sem=rs_recv.at[way, lax.rem(step, depth), i],
+            recv_sem=recv.at[way, lax.rem(step, depth), i],
             device_id={"tp": right if way == 0 else left},
             device_id_type=MESH,
         )
@@ -309,11 +308,22 @@
                 part[turn, 1, i] = term[rows:]
 
     attend_self([last])
+    for i in range(CHUNKS):
+        part[0, 0, i] = jnp.dot(
+            both[:rows, :head],
+            w_out[:head, i * cols : (i + 1) * cols],
+            preferred_element_type=jnp.float32,
+        )
     pltpu.make_async_copy(kv_far, kv_far, kv_recv).wait()
     attend_cross([last])
     for i in (0, 2, 1, 3):
         way = 0 if i < CHUNKS // 2 else 1
-        rs_out[way * half * CHUNKS + i] = expand(rows, i).astype(jnp.bfloat16)
+        term = part[0, 0, i] + jnp.dot(
+            both[:rows, head:],
+            w_out[head:, i * cols : (i + 1) * cols],
+            preferred_element_type=jnp.float32,
+        )
+        rs_out[way * half * CHUNKS + i] = term.astype(jnp.bfloat16)
         scatter_copy(way, 0, i).start()
     for piece in range(4):
         partial_piece(1, [block(half - 1), block(1 - half)], piece)
@@ -396,7 +406,6 @@
             pltpu.SemaphoreType.DMA((3,)),
             pltpu.SemaphoreType.DMA((2, 4, CHUNKS)),
             pltpu.SemaphoreType.DMA,
-            pltpu.SemaphoreType.DMA((2, 4, CHUNKS)),
         ],
         compiler_params=pltpu.CompilerParams(
             collective_id=0, has_side_effects=True, vmem_limit_bytes=56 * 1024 * 1024

time: 163 us -> 163 us (level)
  no operation moved by 1% of the time
where the time goes in v4:
time: 163 us; the launch traced here: 162 us
  Pallas kernels  161 us (99%)
    pallas_call x1, Pallas kernels, local(): pl.pallas_call(functools.partial(kernel, n), out_shape=pltpu.VMEM((rows,...  161 us

profile of v4, /device:TPU:38, one launch (start us, length us, event | category | flops | bytes accessed | tf_op | source)
XLA Modules:
  0.0 161.7 jit_solution(7016709246871138627)
XLA Ops:
  0.0 161.0 %shard_map.82 = bf16[32,3072]{1,0:T(8,128)(2,1)S(1)} custom-call(bf16[32,3072]{1,0:T(8,128)(2,1)} %bitcast.11, f32[3,1,3072]{2,1,0:T(1,128)} %bitcast.12, f32[3,1,128]{2,1,0:T(1,128)} %bitcast.13, f32[1,128]{1,0:T(1,128)} %constant.2.clone.freq_hbm, s32[1,2]{1,0:T(1,128)} %bitcast.14, s32[1,2]{1,0:T(1,128)} %bitcast.15, bf16[12288,128]{1,0:T(8,128)(2,1)} %bitcast.9, ...), custom_call_target="tpu_custom_call" | custom-call | tf_op jit(solution)/shard_map/pallas_call | solution.py:377
  161.1 0.7 copy.10

commit v5 on v4

--- a/solution.py
+++ b/solution.py
@@ -166,11 +166,12 @@
 
     win_copy.wait()
     fold = wide.shape[0] // 4
+    placed = (1, 2, 0, 3)
 
     def unfold(j, carry):
         wide[...] = raw[pl.ds(pl.multiple_of(j * 4 * fold, 4 * fold), 4 * fold), :].astype(jnp.float32)
-        for c in range(4):
-            w_in[pl.ds(pl.multiple_of(j * fold, fold), fold), c * head : (c + 1) * head] = wide[
+        for place, c in enumerate(placed):
+            w_in[pl.ds(pl.multiple_of(j * fold, fold), fold), place * head : (place + 1) * head] = wide[
                 pl.ds(c, fold, stride=4), :
             ].astype(jnp.bfloat16)
         return carry
@@ -186,14 +187,15 @@
     def row_positions(b):
         return offset + b * rows + lax.broadcasted_iota(jnp.int32, (rows, 1), 0)
 
-    def project(i, blocks, first):
+    def project(i, blocks, first, begin=0, end=4):
         picked = [rows_all[b * CHUNKS + i] for b in blocks]
         lhs = picked[0] if len(picked) == 1 else jnp.concatenate(picked, 0)
-        term = jnp.dot(lhs, w_in[i * cols : (i + 1) * cols, :], preferred_element_type=jnp.float32)
+        span = slice(begin * head, end * head)
+        term = jnp.dot(lhs, w_in[i * cols : (i + 1) * cols, span], preferred_element_type=jnp.float32)
         if first:
-            acc[: lhs.shape[0], :] = term
+            acc[: lhs.shape[0], span] = term
         else:
-            acc[: lhs.shape[0], :] += term
+            acc[: lhs.shape[0], span] += term
 
     def prepare_turn(blocks):
         for j, b in enumerate(blocks):
@@ -202,32 +204,34 @@
             trig[0, j * rows : (j + 1) * rows] = jnp.cos(angles)
             trig[1, j * rows : (j + 1) * rows] = jnp.where(is_even, -sine, sine)
 
-    def finish(blocks, send=False):
+    def turned(count, place, g):
+        x = acc[:count, place * head : (place + 1) * head]
+        square = jnp.mean(x * x, -1, keepdims=True)
+        x = x * lax.rsqrt(square + epsilon) * gain_ref[g]
+        swapped = jnp.where(is_even, pltpu.roll(x, head - 1, 1), pltpu.roll(x, 1, 1))
+        return (x * trig[0, :count] + swapped * trig[1, :count]).astype(jnp.bfloat16)
+
+    def finish_pairs(blocks):
         count = len(blocks) * rows
-        cosine = trig[0, :count]
-        sine = trig[1, :count]
-
-        def turned(c, g):
-            x = acc[:count, c * head : (c + 1) * head]
-            square = jnp.mean(x * x, -1, keepdims=True)
-            x = x * lax.rsqrt(square + epsilon) * gain_ref[g]
-            swapped = jnp.where(is_even, pltpu.roll(x, head - 1, 1), pltpu.roll(x, 1, 1))
-            return (x * cosine + swapped * sine).astype(jnp.bfloat16)
-
-        keys = turned(1, 1)
-        values = acc[:count, 2 * head : 3 * head].astype(jnp.bfloat16)
+        keys = turned(count, 0, 1)
+        values = acc[:count, head : 2 * head].astype(jnp.bfloat16)
         for j, b in enumerate(blocks):
             span = slice(j * rows, (j + 1) * rows)
             kv_own[b, 0] = keys[span]
             kv_own[b, 1] = values[span]
-            if send:
-                kv_copy(b).start()
-        queries = turned(0, 0)
-        cross = turned(3, 2)
+
+    def finish_queries(blocks):
+        count = len(blocks) * rows
+        queries = turned(count, 2, 0)
+        cross = turned(count, 3, 2)
         for j, b in enumerate(blocks):
             span = slice(j * rows, (j + 1) * rows)
             q_all[b] = queries[span]
             c_all[b] = cross[span]
+
+    def finish(blocks):
+        finish_pairs(blocks)
+        finish_queries(blocks)
 
     for i in range(CHUNKS):
         project(i, [me], i == 0)
@@ -266,8 +270,15 @@
         for way in range(2):
             i = gather_chunk(way, slot)
             gather_arrival(way, half, i).wait_recv()
-            project(i, [last], slot == 0 and way == 0)
-    finish([last], True)
+            if slot < CHUNKS // 2 - 1:
+                project(i, [last], slot == 0 and way == 0)
+            else:
+                project(i, [last], False, 0, 2)
+    finish_pairs([last])
+    kv_copy(last).start()
+    for way in range(2):
+        project(gather_chunk(way, CHUNKS // 2 - 1), [last], False, 2, 4)
+    finish_queries([last])
 
     def attend(queries, pairs, row):
         keys = pairs[:, 0].reshape(tokens, head)

time: 163 us -> 162 us (level)
  no operation moved by 1% of the time
where the time goes in v5:
time: 162 us
  Pallas kernels  161 us (99%)
    pallas_call x1, Pallas kernels, local(): pl.pallas_call(functools.partial(kernel, n), out_shape=pltpu.VMEM((rows,...  161 us

profile of v5, /device:TPU:38, one launch (start us, length us, event | category | flops | bytes accessed | tf_op | source)
XLA Modules:
  0.0 161.7 jit_solution(7853859265108547558)
XLA Ops:
  0.0 161.0 %shard_map.82 = bf16[32,3072]{1,0:T(8,128)(2,1)S(1)} custom-call(bf16[32,3072]{1,0:T(8,128)(2,1)} %bitcast.11, f32[3,1,3072]{2,1,0:T(1,128)} %bitcast.12, f32[3,1,128]{2,1,0:T(1,128)} %bitcast.13, f32[1,128]{1,0:T(1,128)} %constant.2.clone.freq_hbm, s32[1,2]{1,0:T(1,128)} %bitcast.14, s32[1,2]{1,0:T(1,128)} %bitcast.15, bf16[12288,128]{1,0:T(8,128)(2,1)} %bitcast.9, ...), custom_call_target="tpu_custom_call" | custom-call | tf_op jit(solution)/shard_map/pallas_call | solution.py:388
  161.0 0.7 copy.10

commit v6 on v5

--- a/solution.py
+++ b/solution.py
@@ -107,12 +107,16 @@
     def gather_arrival(way, step, i):
         return gather_copy(way, step - 1, i)
 
-    def kv_copy(b):
+    def place_of(b):
+        return lax.rem(b - me + half - 1 + n, n)
+
+    def kv_copy(b, recv_index=0):
+        place = n - 1 if recv_index else place_of(b)
         return pltpu.make_async_remote_copy(
-            src_ref=kv_own.at[b],
-            dst_ref=kv_far.at[b],
+            src_ref=kv_own.at[place],
+            dst_ref=kv_far.at[place],
             send_sem=out_sem.at[1],
-            recv_sem=kv_recv,
+            recv_sem=kv_recv.at[recv_index],
             device_id={"tower": other},
             device_id_type=MESH,
         )
@@ -139,7 +143,7 @@
             src_ref=ref.at[pl.ds(0, count)],
             dst_ref=ref.at[pl.ds(0, count)],
             send_sem=sem,
-            recv_sem=kv_recv,
+            recv_sem=kv_recv.at[0],
             device_id={"tower": other},
             device_id_type=MESH,
         )
@@ -160,7 +164,9 @@
             gather_copy(way, 0, gather_chunk(way, slot)).start()
 
     cnt_copy.wait()
-    key_index = lax.broadcasted_iota(jnp.int32, (1, tokens), 1)
+    key_index = lax.rem(
+        lax.broadcasted_iota(jnp.int32, (1, tokens), 1) + (me + half + 1) * rows, tokens
+    )
     bias[0:1, :] = jnp.where(key_index < cnt_ref[0, tower], 0.0, masked_score)
     bias[1:2, :] = jnp.where(key_index < cnt_ref[0, other], 0.0, masked_score)
 
@@ -217,8 +223,8 @@
         values = acc[:count, head : 2 * head].astype(jnp.bfloat16)
         for j, b in enumerate(blocks):
             span = slice(j * rows, (j + 1) * rows)
-            kv_own[b, 0] = keys[span]
-            kv_own[b, 1] = values[span]
+            kv_own[place_of(b), 0] = keys[span]
+            kv_own[place_of(b), 1] = values[span]
 
     def finish_queries(blocks):
         count = len(blocks) * rows
@@ -275,7 +281,7 @@
             else:
                 project(i, [last], False, 0, 2)
     finish_pairs([last])
-    kv_copy(last).start()
+    kv_copy(last, 1).start()
     for way in range(2):
         project(gather_chunk(way, CHUNKS // 2 - 1), [last], False, 2, 4)
     finish_queries([last])
@@ -291,6 +297,15 @@
         total = jnp.sum(raised, -1, keepdims=True)
         summed = jnp.dot(raised.astype(jnp.bfloat16), values, preferred_element_type=jnp.float32)
         return (summed / total).astype(jnp.bfloat16)
+
+    def scored(queries, keys, row, begin, end):
+        scores = lax.dot_general(
+            queries,
+            keys.reshape(end - begin, head),
+            (((1,), (1,)), ((), ())),
+            preferred_element_type=jnp.float32,
+        )
+        return scores * score_scale + bias[row : row + 1, begin:end]
 
     def attend_self(blocks):
         picked = [q_all[b] for b in blocks]
@@ -318,15 +333,39 @@
                 part[turn, 0, i] = term[:rows]
                 part[turn, 1, i] = term[rows:]
 
+    pltpu.make_async_copy(
+        kv_far.at[pl.ds(0, n - 1)], kv_far.at[pl.ds(0, n - 1)], kv_recv.at[0]
+    ).wait()
+    split = n - max(128 // rows, 1)
+    cross = c_all[last]
+    early = scored(cross, kv_far[:split, 0], 1, 0, split * rows)
     attend_self([last])
+    early_max = jnp.max(early, -1, keepdims=True)
+    early = jnp.exp2(early - early_max)
+    early_total = jnp.sum(early, -1, keepdims=True)
+    early_sum = jnp.dot(
+        early.astype(jnp.bfloat16),
+        kv_far[:split, 1].reshape(split * rows, head),
+        preferred_element_type=jnp.float32,
+    )
     for i in range(CHUNKS):
         part[0, 0, i] = jnp.dot(
             both[:rows, :head],
             w_out[:head, i * cols : (i + 1) * cols],
             preferred_element_type=jnp.float32,
         )
-    pltpu.make_async_copy(kv_far, kv_far, kv_recv).wait()
-    attend_cross([last])
+    kv_copy(last, 1).wait_recv()
+    late = scored(cross, kv_far[split:, 0], 1, split * rows, tokens)
+    top = jnp.maximum(early_max, jnp.max(late, -1, keepdims=True))
+    late = jnp.exp2(late - top)
+    kept = jnp.exp2(early_max - top)
+    total = kept * early_total + jnp.sum(late, -1, keepdims=True)
+    summed = kept * early_sum + jnp.dot(
+        late.astype(jnp.bfloat16),
+        kv_far[split:, 1].reshape(tokens - split * rows, head),
+        preferred_element_type=jnp.float32,
+    )
+    both[:rows, head:] = (summed / total).astype(jnp.bfloat16)
     for i in (0, 2, 1, 3):
         way = 0 if i < CHUNKS // 2 else 1
         term = part[0, 0, i] + jnp.dot(
@@ -416,7 +455,7 @@
             pltpu.SemaphoreType.DMA((8,)),
             pltpu.SemaphoreType.DMA((3,)),
             pltpu.SemaphoreType.DMA((2, 4, CHUNKS)),
-            pltpu.SemaphoreType.DMA,
+            pltpu.SemaphoreType.DMA((2,)),
         ],
         compiler_params=pltpu.CompilerParams(
             collective_id=0, has_side_effects=True, vmem_limit_bytes=56 * 1024 * 1024

time: 162 us -> 162 us (level)
  no operation moved by 1% of the time
where the time goes in v6:
time: 162 us
  Pallas kernels  161 us (99%)
    pallas_call x1, Pallas kernels, local(): pl.pallas_call(functools.partial(kernel, n), out_shape=pltpu.VMEM((rows,...  161 us

profile of v6, /device:TPU:38, one launch (start us, length us, event | category | flops | bytes accessed | tf_op | source)
XLA Modules:
  0.0 161.7 jit_solution(13910553891982611133)
XLA Ops:
  0.0 161.0 %shard_map.82 = bf16[32,3072]{1,0:T(8,128)(2,1)S(1)} custom-call(bf16[32,3072]{1,0:T(8,128)(2,1)} %bitcast.11, f32[3,1,3072]{2,1,0:T(1,128)} %bitcast.12, f32[3,1,128]{2,1,0:T(1,128)} %bitcast.13, f32[1,128]{1,0:T(1,128)} %constant.2.clone.freq_hbm, s32[1,2]{1,0:T(1,128)} %bitcast.14, s32[1,2]{1,0:T(1,128)} %bitcast.15, bf16[12288,128]{1,0:T(8,128)(2,1)} %bitcast.9, ...), custom_call_target="tpu_custom_call" | custom-call | tf_op jit(solution)/shard_map/pallas_call | solution.py:427
  161.0 0.7 copy.10

commit v7 on v6

--- a/solution.py
+++ b/solution.py
@@ -67,6 +67,10 @@
     tokens = n * rows
     score_scale = math.log2(math.e) / math.sqrt(head)
 
+    barrier = pltpu.get_barrier_semaphore()
+    for where in ({"tp": left}, {"tp": right}, {"tower": other}):
+        pl.semaphore_signal(barrier, inc=1, device_id=where, device_id_type=MESH)
+
     loads = [
         pltpu.make_async_copy(source, target, w_sem.at[j])
         for j, (source, target) in enumerate(
@@ -86,10 +90,6 @@
     for load in loads:
         load.start()
 
-    barrier = pltpu.get_barrier_semaphore()
-    for where in ({"tp": left}, {"tp": right}, {"tower": other}):
-        pl.semaphore_signal(barrier, inc=1, device_id=where, device_id_type=MESH)
-
     def block(offset):
         return lax.rem(me + offset + 2 * n, n)
 
@@ -153,15 +153,21 @@
     states = h_ref[...].astype(jnp.float32)
     centre = states - jnp.mean(states, -1, keepdims=True)
     spread = jnp.mean(centre * centre, -1, keepdims=True)
-    normed = centre * lax.rsqrt(spread + epsilon) * (1.0 + mod_ref[1]) + mod_ref[0]
-    normed = normed.astype(jnp.bfloat16)
-    for i in range(CHUNKS):
-        rows_all[me * CHUNKS + i] = normed[:, i * cols : (i + 1) * cols]
-
+    inverse = lax.rsqrt(spread + epsilon)
+
+    def normalize(i):
+        span = slice(i * cols, (i + 1) * cols)
+        normed = centre[:, span] * inverse * (1.0 + mod_ref[1, :, span]) + mod_ref[0, :, span]
+        rows_all[me * CHUNKS + i] = normed.astype(jnp.bfloat16)
+
+    for way in range(2):
+        normalize(gather_chunk(way, 0))
     pl.semaphore_wait(barrier, 3)
     for slot in range(CHUNKS):
         for way in range(2):
             gather_copy(way, 0, gather_chunk(way, slot)).start()
+            if slot + 1 < CHUNKS // 2:
+                normalize(gather_chunk(way, slot + 1))
 
     cnt_copy.wait()
     key_index = lax.rem(

time: 162 us -> 162 us (level)
  no operation moved by 1% of the time
where the time goes in v7:
time: 162 us
  Pallas kernels  161 us (99%)
    pallas_call x1, Pallas kernels, local(): pl.pallas_call(functools.partial(kernel, n), out_shape=pltpu.VMEM((rows,...  161 us

profile of v7, /device:TPU:38, one launch (start us, length us, event | category | flops | bytes accessed | tf_op | source)
XLA Modules:
  0.0 161.7 jit_solution(2214158572316128021)
XLA Ops:
  0.0 161.0 %shard_map.82 = bf16[32,3072]{1,0:T(8,128)(2,1)S(1)} custom-call(bf16[32,3072]{1,0:T(8,128)(2,1)} %bitcast.11, f32[3,1,3072]{2,1,0:T(1,128)} %bitcast.12, f32[3,1,128]{2,1,0:T(1,128)} %bitcast.13, f32[1,128]{1,0:T(1,128)} %constant.2.clone.freq_hbm, s32[1,2]{1,0:T(1,128)} %bitcast.14, s32[1,2]{1,0:T(1,128)} %bitcast.15, bf16[12288,128]{1,0:T(8,128)(2,1)} %bitcast.9, ...), custom_call_target="tpu_custom_call" | custom-call | tf_op jit(solution)/shard_map/pallas_call | solution.py:433
  161.0 0.7 copy.10

commit v8 on v7

--- a/solution.py
+++ b/solution.py
@@ -252,7 +252,6 @@
 
     def gather_step(step, carry):
         before, after = block(-step), block(step)
-        prepare_turn([before, after])
         for slot in range(CHUNKS):
             for way in range(2):
                 i = gather_chunk(way, slot)
@@ -264,6 +263,7 @@
             if slot == 0:
                 kv_copy(block(1 - step)).start()
                 pl.when(step > 1)(lambda: kv_copy(block(step - 1)).start())
+                prepare_turn([before, after])
             if slot >= CHUNKS // 2:
                 project(gather_chunk(0, slot), [before, after], slot == CHUNKS // 2)
                 project(gather_chunk(1, slot), [before, after], False)

time: 162 us -> 162 us (level)
  no operation moved by 1% of the time
where the time goes in v8:
time: 162 us
  Pallas kernels  161 us (99%)
    pallas_call x1, Pallas kernels, local(): pl.pallas_call(functools.partial(kernel, n), out_shape=pltpu.VMEM((rows,...  161 us

profile of v8, /device:TPU:38, one launch (start us, length us, event | category | flops | bytes accessed | tf_op | source)
XLA Modules:
  0.0 161.5 jit_solution(9961682914548828631)
XLA Ops:
  0.0 160.9 %shard_map.82 = bf16[32,3072]{1,0:T(8,128)(2,1)S(1)} custom-call(bf16[32,3072]{1,0:T(8,128)(2,1)} %bitcast.11, f32[3,1,3072]{2,1,0:T(1,128)} %bitcast.12, f32[3,1,128]{2,1,0:T(1,128)} %bitcast.13, f32[1,128]{1,0:T(1,128)} %constant.2.clone.freq_hbm, s32[1,2]{1,0:T(1,128)} %bitcast.14, s32[1,2]{1,0:T(1,128)} %bitcast.15, bf16[12288,128]{1,0:T(8,128)(2,1)} %bitcast.9, ...), custom_call_target="tpu_custom_call" | custom-call | tf_op jit(solution)/shard_map/pallas_call | solution.py:433
  160.9 0.7 copy.10
